TPU v7x, 32 devices: a whole 2x2x4 slice. The times are simulated.
32 devices in a mesh: dp: 8 (over z, y), tensor: 4 (over x, core).
Axes of the slice: x: 2, y: 2, z: 4, core: 2. Of those that a mesh axis runs over, the one named last changes fastest.
Arguments:
- grads: bfloat16 [8, 1024, 28672], P('dp', None, 'tensor'), may hold values from -6 to 6
- errors: bfloat16 [8, 1024, 28672], P('dp', None, 'tensor'), may hold values from -4 to 4
- basis: float32 [28672, 32], P('tensor'), may hold values from -6 to 6
Outputs:
- new_errors: bfloat16 [8, 1024, 28672], P('dp', None, 'tensor')
- p_basis: float32 [1024, 32], P('tensor')
- q_basis: float32 [28672, 32], P('tensor')
All inputs are finite; a program needn't handle non-finite values.
Results may differ from a plain program's by a relative error of at most 0.014.
Values may be sent and summed in bfloat16 or wider, within the bound.
A program may use at most 128 MiB of HBM per device.

v0:
```python
import jax
import jax.numpy as jnp
from jax import lax
from jax.sharding import PartitionSpec as P


def orthonormal(p_rows, gram):
    lower = jnp.linalg.cholesky(gram)
    return jax.scipy.linalg.solve_triangular(lower, p_rows.T, lower=True).T


def on_device(grads, errors, basis):
    matrix = (grads[0].astype(jnp.float32) + errors[0].astype(jnp.float32)).astype(jnp.bfloat16)
    partial_p = jnp.dot(matrix, basis.astype(jnp.bfloat16), preferred_element_type=jnp.float32)
    p_block = lax.psum_scatter(partial_p, "tensor", scatter_dimension=0, tiled=True)
    p_block = lax.psum(p_block, "dp")
    local_gram = jnp.dot(p_block.T, p_block, precision=lax.Precision.HIGHEST)
    gram = lax.psum(local_gram, "tensor")
    p_basis = orthonormal(p_block, gram)
    p_b = lax.all_gather(p_basis.astype(jnp.bfloat16), "tensor", axis=0, tiled=True)
    local_q = lax.dot_general(
        matrix, p_b, (((0,), (0,)), ((), ())), preferred_element_type=jnp.float32
    )
    q_basis = lax.psum(local_q.astype(jnp.bfloat16), "dp").astype(jnp.float32) / lax.axis_size("dp")
    approx = jnp.dot(p_b, q_basis.astype(jnp.bfloat16).T, preferred_element_type=jnp.float32)
    new_errors = (matrix.astype(jnp.float32) - approx).astype(jnp.bfloat16)[None]
    return (new_errors, p_basis, q_basis)


def solution(mesh):
    return jax.shard_map(
        on_device,
        mesh=mesh,
        in_specs=(P("dp", None, "tensor"), P("dp", None, "tensor"), P("tensor", None)),
        out_specs=(P("dp", None, "tensor"), P("tensor", None), P("tensor", None)),
        check_vma=False,
    )
```

profile of v0, /device:TPU:0, one launch (start us, length us, event | category | flops | bytes accessed | tf_op | source)
XLA Modules:
  0.0 211.5 jit_solution(11256117579849743705)
XLA Ops:
  7.2 0.0 reduce-scatter.2.cloned.1.call-start
  7.2 14.6 %fusion.3 = f32[1024,32]{0,1:T(8,128)} fusion(f32[7168,32]{0,1:T(8,128)} %param.5, bf16[1,1024,7168]{2,1,0:T(8,128)(2,1)} %param.4, bf16[1,1024,7168]{2,1,0:T(8,128)(2,1)} %param.3), kind=kOutput, calls=%fused_computation.7 | convolution fusion | flops 499351552 | bytes 30408704 | tf_op jit(solution)/shard_map/dot_general | solution.py:14
  21.8 0.0 reduce-scatter.2.cloned.1.call-update
  21.8 0.0 all-reduce.2.cloned.1.call-start
  21.9 22.5 %reduce-scatter.2.cloned.1.call-done = f32[256,32]{0,1:T(8,128)} async-done(((f32[1024,32]{0,1:T(8,128)}), f32[256,32]{0,1:T(8,128)}) %reduce-scatter.2.cloned.1.call-update) | async-done | bytes 32784 | tf_op jit(solution)/shard_map/reduce_scatter | solution.py:15
  44.4 37.7 %psum.21 = f32[256,32]{0,1:T(8,128)S(1)} all-reduce(f32[256,32]{0,1:T(8,128)} %reduce-scatter.2.cloned.1.call-done), channel_id=1, replica_groups=mesh['dp'=8,'tensor'=4] {'dp'}, use_global_device_ids=true, to_apply=%region_1.0 | all-reduce | flops 8192 | bytes 65536 | tf_op jit(solution)/shard_map/psum | solution.py:16
  82.1 0.2 fusion.12
  82.3 10.2 %psum.22 = f32[32,32]{0,1:T(8,128)S(1)} all-reduce(f32[32,32]{0,1:T(8,128)S(1)} %fusion.12), channel_id=1, replica_groups=mesh['dp'=8,'tensor'=4] {'tensor'}, use_global_device_ids=true, to_apply=%region_2.0 | all-reduce | flops 1024 | bytes 8192 | tf_op jit(solution)/shard_map/psum | solution.py:18
  92.5 0.1 copy.7
  92.6 2.9 %cholesky.16 = f32[32,32]{1,0:T(8,128)S(1)} custom-call(f32[32,32]{1,0:T(8,128)S(1)} %fusion.8), custom_call_target="Cholesky" | custom-call | tf_op jit(solution)/shard_map/jit(cholesky)/cholesky | solution.py:8
  95.6 0.6 compare_reduce_fusion
  96.2 0.7 fusion.5
  96.9 2.4 %custom-call.7 = f32[1,32,32]{1,2,0:T(8,128)S(1)} custom-call(f32[1,32,32]{2,1,0:T(8,128)S(1)} %fusion.5), custom_call_target="InvertDiagBlocksLowerTriangular" | custom-call | tf_op jit(solution)/shard_map/jit(_solve_triangular)/triangular_solve | solution.py:9
  99.3 0.9 fusion.11
  100.2 5.2 %all_gather.3 = bf16[1024,32]{0,1:T(8,128)(2,1)S(1)} all-gather(bf16[256,32]{0,1:T(8,128)(2,1)S(1)} %get-tuple-element.3), channel_id=1, replica_groups=mesh['dp'=8,'tensor'=4] {'tensor'}, dimensions={0}, use_global_device_ids=true | all-gather | bytes 81920 | tf_op jit(solution)/shard_map/all_gather | solution.py:20
  105.4 12.2 %convolution_convert_fusion = bf16[7168,32]{0,1:T(8,128)(2,1)} fusion(bf16[1024,32]{0,1:T(8,128)(2,1)S(1)} %all_gather.3, bf16[1,1024,7168]{2,1,0:T(8,128)(2,1)} %param.4, bf16[1,1024,7168]{2,1,0:T(8,128)(2,1)} %param.3), kind=kOutput, calls=%fused_computation.4 | convolution fusion | flops 499351552 | bytes 29884416 | tf_op jit(solution)/shard_map/dot_general | solution.py:21
  117.6 0.0 all-reduce.2.cloned.1.call-update
  117.6 68.7 %all-reduce.2.cloned.1.call-done = bf16[7168,32]{0,1:T(8,128)(2,1)} async-done(((bf16[7168,32]{0,1:T(8,128)(2,1)}), bf16[7168,32]{0,1:T(8,128)(2,1)}) %all-reduce.2.cloned.1.call-update) | async-done | bytes 458768 | tf_op jit(solution)/shard_map/psum | solution.py:24
  186.4 1.1 convert_multiply_fusion
  187.4 0.0 copy-start
  187.4 17.2 %fusion.1 = bf16[1,1024,7168]{2,1,0:T(8,128)(2,1)} fusion(bf16[1024,32]{0,1:T(8,128)(2,1)S(1)} %all_gather.3, f32[7168,32]{0,1:T(8,128)S(1)} %convert_multiply_fusion, bf16[1,1024,7168]{2,1,0:T(8,128)(2,1)} %param.4, bf16[1,1024,7168]{2,1,0:T(8,128)(2,1)} %param.3), kind=kOutput, calls=%fused_computation.3 | convolution fusion | flops 521371648 | bytes 45023232 | tf_op jit(solution)/shard_map/dot_general | solution.py:25
  204.7 0.0 copy-done
  (2 shorter events, 0.0 us)
Async XLA Ops:
  7.2 37.2 %reduce-scatter.2.cloned.1.call-start = ((), (), s32[]{:S(2)}) async-start(), calls=%async_computation.1 | async-start | bytes 163840 | tf_op jit(solution)/shard_map/reduce_scatter | solution.py:15
  21.8 164.5 %all-reduce.2.cloned.1.call-start = ((), (), s32[]{:S(2)}) async-start(), calls=%async_computation.2 | async-start | bytes 917504 | tf_op jit(solution)/shard_map/psum | solution.py:24
  187.4 17.3 %copy-start = (f32[7168,32]{0,1:T(8,128)}, f32[7168,32]{0,1:T(8,128)S(1)}, u32[]{:S(2)}) copy-start(f32[7168,32]{0,1:T(8,128)S(1)} %convert_multiply_fusion) | copy-start | bytes 2752516
Sparse Core Ops, SparseCore 0:
  22.0 22.3 reduce-scatter.1
  117.8 68.5 all-reduce.1
where the time goes:
time: 212 us
  waiting for transfers between devices  91.2 us (43%)
  blocking collectives  53.2 us (25%)
  matrix products  45.1 us (21%)
  between operations  14.1 us (7%)
  other arithmetic  7.77 us (4%)
    psum x1, waiting for transfers between devices, on_device(): lax.psum(local_q.astype(jnp.bfloat16), 'dp').astype(jnp.float32)  68.7 us
    psum x1, blocking collectives, on_device(): p_block = lax.psum(p_block, 'dp')  37.7 us
    reduce_scatter x1, waiting for transfers between devices, on_device(): lax.psum_scatter(partial_p, 'tensor', scatter_dimension=0, tiled=True)  22.5 us
    dot_general x1, matrix products, on_device(): jnp.dot(p_b, q_basis.astype(jnp.bfloat16).T, preferred_element_type=jnp.f...  17.2 us
    dot_general x1, matrix products, on_device(): jnp.dot(matrix, basis.astype(jnp.bfloat16), preferred_element_type=jnp.fl...  14.6 us
    dot_general x1, matrix products, on_device(): lax.dot_general(matrix, p_b, (((0,), (0,)), ((), ())), preferred_element_...  12.2 us
    psum x1, blocking collectives, on_device(): gram = lax.psum(local_gram, 'tensor')  10.2 us
    all_gather x1, blocking collectives, on_device(): lax.all_gather(p_basis.astype(jnp.bfloat16), 'tensor', axis=0, tiled=True)  5.22 us
  transfers between devices with their start and end apart: 2, of which 2 were waited for; matrix products, arithmetic and copies ran while one was open for 0% of the time, Pallas kernels for 0%

commit v1 on v0

--- a/solution.py
+++ b/solution.py
@@ -1,7 +1,16 @@
+import functools
+
 import jax
 import jax.numpy as jnp
 from jax import lax
+from jax.experimental import pallas as pl
+from jax.experimental.pallas import tpu as pltpu
 from jax.sharding import PartitionSpec as P
+
+F32, BF16 = jnp.float32, jnp.bfloat16
+MESH = pl.DeviceIdType.MESH
+HIGHEST = lax.Precision.HIGHEST
+LANES = 128
 
 
 def orthonormal(p_rows, gram):
@@ -9,7 +18,7 @@
     return jax.scipy.linalg.solve_triangular(lower, p_rows.T, lower=True).T
 
 
-def on_device(grads, errors, basis):
+def plain_on_device(grads, errors, basis):
     matrix = (grads[0].astype(jnp.float32) + errors[0].astype(jnp.float32)).astype(jnp.bfloat16)
     partial_p = jnp.dot(matrix, basis.astype(jnp.bfloat16), preferred_element_type=jnp.float32)
     p_block = lax.psum_scatter(partial_p, "tensor", scatter_dimension=0, tiled=True)
@@ -27,9 +36,350 @@
     return (new_errors, p_basis, q_basis)
 
 
+def ds(start, size, align):
+    return pl.ds(pl.multiple_of(start, align), size)
+
+
+def dot(a, b, dims, precision=None):
+    return lax.dot_general(a, b, (dims, ((), ())), precision=precision, preferred_element_type=F32)
+
+
+def inverse_factor(gram):
+    n = gram.shape[0]
+    rows = lax.broadcasted_iota(jnp.int32, (n, n), 0)
+    cols = lax.broadcasted_iota(jnp.int32, (n, n), 1)
+    inv = jnp.where(rows == cols, 1.0, 0.0).astype(F32)
+    for k in range(n - 1):
+        column = jnp.broadcast_to(gram[:, k : k + 1], (n, n))
+        factor = jnp.where(rows > k, column / column[k : k + 1, :], 0.0)
+        gram = gram - factor * gram[k : k + 1, :]
+        inv = inv - factor * inv[k : k + 1, :]
+    pivots = jnp.sum(jnp.where(rows == cols, gram, 0.0), axis=1, keepdims=True)
+    return inv / jnp.sqrt(pivots)
+
+
+def exchange_kernel(
+    n_dp, n_t,
+    grads, errors, basis_t,
+    matrix, p_out, q_out,
+    err, basis_b, p_send, p_recv, t_buf, g_buf, pb,
+    y_send, y_recv, own, z_send, z_recv, q_all,
+    g_in, e_in, ps_s, ps_r, t_s, t_r, g_s, g_r, y_s, y_r, z_s, z_r, a_s, a_r, f_s, f_r,
+):
+    d, t = lax.axis_index("dp"), lax.axis_index("tensor")
+    rank, ff = basis_t.shape
+    rows = matrix.shape[0]
+    block = rows // n_dp
+    piece = ff // n_dp
+    half = n_dp // 2
+    hi, lo = d // 2, lax.rem(d, 2)
+    mate = hi * 2 + 1 - lo
+
+    def nth(i, me, n):
+        return lax.rem(me + 1 + i, n)
+
+    def load(j):
+        at = ds(j * block, block, block)
+        return (
+            pltpu.make_async_copy(grads.at[at, :], matrix.at[at, :], g_in.at[j]),
+            pltpu.make_async_copy(errors.at[at, :], err.at[at, :], e_in.at[j]),
+        )
+
+    @pl.loop(0, n_dp)
+    def _(i):
+        for copy in load(nth(i, d, n_dp)):
+            copy.start()
+
+    barrier = pltpu.get_barrier_semaphore()
+
+    @pl.loop(0, n_dp - 1)
+    def _(i):
+        pl.semaphore_signal(barrier, inc=1, device_id=(nth(i, d, n_dp), t), device_id_type=MESH)
+
+    @pl.loop(0, n_t - 1)
+    def _(i):
+        pl.semaphore_signal(barrier, inc=1, device_id=(d, nth(i, t, n_t)), device_id_type=MESH)
+
+    basis_b[...] = basis_t[...].astype(BF16)
+    pl.semaphore_wait(barrier, n_dp + n_t - 2)
+
+    def remote(src, dst, send, recv, dp, tensor):
+        return pltpu.make_async_remote_copy(
+            src_ref=src, dst_ref=dst, send_sem=send, recv_sem=recv,
+            device_id=(dp, tensor), device_id_type=MESH,
+        )
+
+    def partial(j):
+        for copy in load(j):
+            copy.wait()
+        at = ds(j * block, block, block)
+        matrix[at, :] = matrix[at, :] + err[at, :]
+        return dot(basis_b[...], matrix[at, :], ((1,), (1,)))
+
+    def p_copy(j, slot):
+        return remote(p_send.at[j], p_recv.at[slot], ps_s.at[j], ps_r.at[slot], j, t)
+
+    @pl.loop(0, n_dp - 1)
+    def _(i):
+        j = nth(i, d, n_dp)
+        p_send[j] = partial(j)
+        p_copy(j, d).start()
+
+    p_recv[d] = partial(d)
+
+    @pl.loop(0, n_dp - 1)
+    def _(i):
+        j = nth(i, d, n_dp)
+        p_copy(j, j).wait_recv()
+
+    total = p_recv[0]
+    for j in range(1, n_dp):
+        total = total + p_recv[j]
+    t_buf[t] = total
+
+    def t_copy(k, slot):
+        return remote(t_buf.at[t], t_buf.at[slot], t_s.at[k], t_r.at[slot], d, k)
+
+    @pl.loop(0, n_t - 1)
+    def _(i):
+        t_copy(nth(i, t, n_t), t).start()
+
+    @pl.loop(0, n_t - 1)
+    def _(i):
+        k = nth(i, t, n_t)
+        remote(t_buf.at[k], t_buf.at[k], t_s.at[k], t_r.at[k], d, k).wait_recv()
+
+    total = t_buf[0]
+    for k in range(1, n_t):
+        total = total + t_buf[k]
+    g_buf[d] = total
+
+    def g_copy(j, slot):
+        return remote(g_buf.at[slot], g_buf.at[slot], g_s.at[j], g_r.at[slot], j, t)
+
+    @pl.loop(0, n_dp - 1)
+    def _(i):
+        g_copy(nth(i, d, n_dp), d).start()
+
+    @pl.loop(0, n_dp - 1)
+    def _(i):
+        j = nth(i, d, n_dp)
+        g_copy(j, j).wait_recv()
+
+    gram = dot(g_buf[0], g_buf[0], ((1,), (1,)), HIGHEST)
+    for j in range(1, n_dp):
+        gram = gram + dot(g_buf[j], g_buf[j], ((1,), (1,)), HIGHEST)
+    inv = inverse_factor(gram)
+    for j in range(n_dp):
+        p_rows = dot(inv, g_buf[j], ((1,), (0,)), HIGHEST)
+        p_out[:, j * block : (j + 1) * block] = p_rows
+        pb[:, j * block : (j + 1) * block] = p_rows.astype(BF16)
+
+    def q_piece(k):
+        return dot(pb[...], matrix[:, ds(k * piece, piece, LANES)], ((1,), (0,)))
+
+    def y_copy(h):
+        return remote(y_send.at[h], y_recv.at[h], y_s.at[h], y_r.at[h], mate, t)
+
+    def z_copy(h, slot):
+        return remote(z_send.at[h], z_recv.at[slot], z_s.at[h], z_r.at[slot], h * 2 + lo, t)
+
+    def a_copy(h, slot):
+        return remote(q_all.at[slot], q_all.at[slot], a_s.at[h], a_r.at[slot // 2], h * 2 + lo, t)
+
+    def f_copy(slot):
+        return remote(q_all.at[slot], q_all.at[slot], f_s.at[slot // 2], f_r.at[slot // 2], mate, t)
+
+    @pl.loop(0, half)
+    def _(i):
+        h = nth(i, hi, half)
+        y_send[h] = q_piece(h * 2 + 1 - lo).astype(BF16)
+        y_copy(h).start()
+
+    @pl.loop(0, half)
+    def _(i):
+        h = nth(i, hi, half)
+        own[h] = q_piece(h * 2 + lo)
+
+    @pl.loop(0, half - 1)
+    def _(i):
+        h = nth(i, hi, half)
+        y_copy(h).wait_recv()
+        z_send[h] = (own[h] + y_recv[h].astype(F32)).astype(BF16)
+        z_copy(h, hi).start()
+
+    y_copy(hi).wait_recv()
+    own[hi] = own[hi] + y_recv[hi].astype(F32)
+
+    @pl.loop(0, half - 1)
+    def _(i):
+        h = nth(i, hi, half)
+        z_copy(h, h).wait_recv()
+        own[hi] = own[hi] + z_recv[h].astype(F32)
+
+    q_all[d] = (own[hi] / n_dp).astype(BF16)
+
+    @pl.loop(0, half - 1)
+    def _(i):
+        a_copy(nth(i, hi, half), d).start()
+
+    f_copy(d).start()
+
+    @pl.loop(0, half - 1)
+    def _(i):
+        h = nth(i, hi, half)
+        a_copy(h, h * 2 + lo).wait_recv()
+        f_copy(h * 2 + lo).start()
+
+    @pl.loop(0, half)
+    def _(h):
+        f_copy(h * 2 + 1 - lo).wait_recv()
+
+    for j in range(n_dp):
+        q_out[:, j * piece : (j + 1) * piece] = q_all[j]
+
+    @pl.loop(0, n_dp - 1)
+    def _(i):
+        j = nth(i, d, n_dp)
+        p_copy(j, d).wait_send()
+        g_copy(j, d).wait_send()
+
+    @pl.loop(0, n_t - 1)
+    def _(i):
+        t_copy(nth(i, t, n_t), t).wait_send()
+
+    @pl.loop(0, half - 1)
+    def _(i):
+        h = nth(i, hi, half)
+        z_copy(h, hi).wait_send()
+        a_copy(h, d).wait_send()
+
+    @pl.loop(0, half)
+    def _(h):
+        y_copy(h).wait_send()
+        f_copy(h * 2 + lo).wait_send()
+
+
+def output_kernel(n_t, matrix, p_t, q_t, new_errors, p_out, q_out, pb, slots, sems):
+    t = lax.axis_index("tensor")
+    rows, ff = matrix.shape
+    n_slots, _, width = slots.shape
+    chunks = ff // width
+    tile = 128
+    pb[...] = p_t[...].T.astype(BF16)
+
+    def out(i):
+        slot = lax.rem(i, n_slots)
+        return pltpu.make_async_copy(
+            slots.at[slot], new_errors.at[:, ds(i * width, width, LANES)], sems.at[slot]
+        )
+
+    @pl.loop(0, chunks)
+    def _(i):
+        @pl.when(i >= n_slots)
+        def _():
+            out(i - n_slots).wait()
+
+        slot = lax.rem(i, n_slots)
+        columns = ds(i * width, width, LANES)
+
+        @pl.loop(0, rows // tile)
+        def _(r):
+            at = ds(r * tile, tile, tile)
+            approx = dot(pb[at, :], q_t[:, columns], ((1,), (0,)))
+            slots[slot, at, :] = (matrix[at, columns].astype(F32) - approx).astype(BF16)
+
+        out(i).start()
+
+    q_out[...] = q_t[...].astype(F32)
+    mine = rows // n_t
+    p_out[...] = p_t[:, ds(t * mine, mine, LANES)]
+
+    @pl.loop(chunks - n_slots, chunks)
+    def _(i):
+        out(i).wait()
+
+
+def on_device(n_dp, n_t, grads, errors, basis):
+    _, rows, ff = grads.shape
+    rank = basis.shape[1]
+    block, piece, half = rows // n_dp, ff // n_dp, n_dp // 2
+    vmem = pl.BlockSpec(memory_space=pltpu.VMEM)
+    hbm = pl.BlockSpec(memory_space=pl.ANY)
+    dma = lambda n: pltpu.SemaphoreType.DMA((n,))
+    matrix, p_t, q_t = pl.pallas_call(
+        functools.partial(exchange_kernel, n_dp, n_t),
+        name="exchange",
+        out_shape=(
+            pltpu.VMEM((rows, ff), BF16),
+            pltpu.VMEM((rank, rows), F32),
+            pltpu.VMEM((rank, ff), BF16),
+        ),
+        in_specs=[hbm, hbm, vmem],
+        out_specs=(vmem, vmem, vmem),
+        scratch_shapes=[
+            pltpu.VMEM((rows, ff), BF16),
+            pltpu.VMEM((rank, ff), BF16),
+            pltpu.VMEM((n_dp, rank, block), F32),
+            pltpu.VMEM((n_dp, rank, block), F32),
+            pltpu.VMEM((n_t, rank, block), F32),
+            pltpu.VMEM((n_dp, rank, block), F32),
+            pltpu.VMEM((rank, rows), BF16),
+            pltpu.VMEM((half, rank, piece), BF16),
+            pltpu.VMEM((half, rank, piece), BF16),
+            pltpu.VMEM((half, rank, piece), F32),
+            pltpu.VMEM((half, rank, piece), BF16),
+            pltpu.VMEM((half, rank, piece), BF16),
+            pltpu.VMEM((n_dp, rank, piece), BF16),
+            dma(n_dp), dma(n_dp),
+            dma(n_dp), dma(n_dp),
+            dma(n_t), dma(n_t),
+            dma(n_dp), dma(n_dp),
+            dma(half), dma(half),
+            dma(half), dma(half),
+            dma(half), dma(half),
+            dma(half), dma(half),
+        ],
+        compiler_params=pltpu.CompilerParams(
+            collective_id=0, has_side_effects=True, vmem_limit_bytes=36 * 2**20
+        ),
+    )(grads[0], errors[0], basis.T)
+    width = piece
+    n_slots = min(4, ff // width)
+    new_errors, p_mine, q_full = pl.pallas_call(
+        functools.partial(output_kernel, n_t),
+        name="output",
+        out_shape=(
+            jax.ShapeDtypeStruct((rows, ff), BF16),
+            jax.ShapeDtypeStruct((rank, rows // n_t), F32),
+            jax.ShapeDtypeStruct((rank, ff), F32),
+        ),
+        in_specs=[vmem, vmem, vmem],
+        out_specs=(hbm, vmem, vmem),
+        scratch_shapes=[
+            pltpu.VMEM((rows, rank), BF16),
+            pltpu.VMEM((n_slots, rows, width), BF16),
+            dma(n_slots),
+        ],
+        compiler_params=pltpu.CompilerParams(vmem_limit_bytes=16 * 2**20),
+    )(matrix, p_t, q_t)
+    return new_errors[None], p_mine.T, q_full.T
+
+
+def body(n_dp, n_t):
+    def run(grads, errors, basis):
+        _, rows, ff = grads.shape
+        fits = n_dp % 2 == 0 and rows % (n_dp * LANES) == 0 and rows % (n_t * LANES) == 0
+        if fits and ff % (n_dp * LANES) == 0:
+            return on_device(n_dp, n_t, grads, errors, basis)
+        return plain_on_device(grads, errors, basis)
+
+    return run
+
+
 def solution(mesh):
     return jax.shard_map(
-        on_device,
+        body(mesh.shape["dp"], mesh.shape["tensor"]),
         mesh=mesh,
         in_specs=(P("dp", None, "tensor"), P("dp", None, "tensor"), P("tensor", None)),
         out_specs=(P("dp", None, "tensor"), P("tensor", None), P("tensor", None)),

time: 212 us -> 65.8 us (0.31)
  waiting for transfers between devices: 91.2 us -> 0 us
  Pallas kernels: 0 us -> 63.8 us
  blocking collectives: 53.2 us -> 0 us
  matrix products: 45.1 us -> 0 us
  between operations: 14.1 us -> 0.65 us
  other arithmetic: 7.77 us -> 0 us
    psum x1 -> x0, waiting for transfers between devices: 68.7 us -> none  [on_device(): lax.psum(local_q.astype(jnp.bfloat16), 'dp').astype(jnp.float32)]
    pallas_call x0 -> x2, Pallas kernels: none -> 63.8 us  [the longest x1 49 us: on_device(): pl.pallas_call(functools.partial(exchange_kernel, n_dp, n_t), name='excha...]
    psum x2 -> x0, blocking collectives: 48 us -> none  [the longest x1 37.7 us: on_device(): p_block = lax.psum(p_block, 'dp')]
    dot_general x4 -> x0, matrix products: 44.3 us -> none  [the longest x1 17.2 us: on_device(): jnp.dot(p_b, q_basis.astype(jnp.bfloat16).T, preferred_element_type=jnp.f...]
    reduce_scatter x1 -> x0, waiting for transfers between devices: 22.5 us -> none  [on_device(): lax.psum_scatter(partial_p, 'tensor', scatter_dimension=0, tiled=True)]
    another operation x5 -> x0, other arithmetic: 6.68 us -> none  [the longest x3 3.59 us: orthonormal(): lower = jnp.linalg.cholesky(gram)]
    all_gather x1 -> x0, blocking collectives: 5.22 us -> none  [on_device(): lax.all_gather(p_basis.astype(jnp.bfloat16), 'tensor', axis=0, tiled=True)]
  transfers between devices with their start and end apart: 2 -> 0, of which waited for: 2 -> 0; matrix products, arithmetic and copies ran while one was open for 0% -> 0% of each run, Pallas kernels for 0% -> 0%
where the time goes in v1:
time: 65.8 us; the launch traced here: 65.6 us
  Pallas kernels  63.8 us (97%)
  local copies, waits for them, and re-layouts  1.17 us (2%)
    pallas_call x1, Pallas kernels, on_device(): pl.pallas_call(functools.partial(exchange_kernel, n_dp, n_t), name='excha...  49 us
    pallas_call x1, Pallas kernels, on_device(): pl.pallas_call(functools.partial(output_kernel, n_t), name='output', out_...  14.8 us

profile of v1, /device:TPU:0, one launch (start us, length us, event | category | flops | bytes accessed | tf_op | source)
XLA Modules:
  0.0 65.6 jit_solution(10732852669242650726)
XLA Ops:
  0.6 0.0 copy-start
  0.6 1.2 %copy-done = f32[7168,32]{0,1:T(8,128)S(1)} copy-done((f32[7168,32]{0,1:T(8,128)S(1)}, f32[7168,32]{0,1:T(8,128)}, u32[]{:S(2)}) %copy-start) | copy-done | bytes 917528
  1.8 49.0 %exchange.1 = (bf16[1024,7168]{1,0:T(8,128)(2,1)S(1)}, f32[32,1024]{1,0:T(8,128)S(1)}, bf16[32,7168]{1,0:T(8,128)(2,1)S(1)}) custom-call(bf16[1024,7168]{1,0:T(8,128)(2,1)} %bitcast.7, bf16[1024,7168]{1,0:T(8,128)(2,1)} %bitcast.8, f32[32,7168]{1,0:T(8,128)S(1)} %bitcast.6), custom_call_target="tpu_custom_call" | custom-call | tf_op jit(solution)/shard_map/exchange/pallas_call | solution.py:310
  50.8 14.8 %output.1 = (bf16[1024,7168]{1,0:T(8,128)(2,1)}, f32[32,256]{1,0:T(8,128)}, f32[32,7168]{1,0:T(8,128)}) custom-call(bf16[1024,7168]{1,0:T(8,128)(2,1)S(1)} %get-tuple-element.9.matrix, f32[32,1024]{1,0:T(8,128)S(1)} %get-tuple-element.10.p_t, bf16[32,7168]{1,0:T(8,128)(2,1)S(1)} %get-tuple-element.11.q_t), custom_call_target="tpu_custom_call" | custom-call | tf_op jit(solution)/shard_map/output/pallas_call | solution.py:349
Async XLA Ops:
  0.6 1.2 %copy-start = (f32[7168,32]{0,1:T(8,128)S(1)}, f32[7168,32]{0,1:T(8,128)}, u32[]{:S(2)}) copy-start(f32[7168,32]{0,1:T(8,128)} %param.5) | copy-start | bytes 2752516
